TPU v7x, 32 devices: a whole 2x2x4 slice. The times are simulated.
32 devices in a mesh: blk: 8 (over y, x, core), grp: 4 (over z).
Axes of the slice: x: 2, y: 2, z: 4, core: 2. Of those that a mesh axis runs over, the one named last changes fastest.
Arguments:
- samples: float32 [32, 128, 256], P('blk', 'grp'), may hold values from -11 to 11
- pair_table: int32 [32, 16], P('blk'), may hold values from 0 to 31
- assignment: int32 [2, 32], P(None, 'blk'), may hold values from 0 to 127
- band_index: int32 [2], replicated, may hold values from 0 to 1023
Outputs:
- log_weight: float32 [2, 32, 128], P(None, 'blk', 'grp')
All inputs are finite; a program needn't handle non-finite values.
Results may differ from a plain program's by a relative error of at most 0.0003.
Values sent between devices are 32-bit elements; how exact they have to be, the bound alone decides.
No kernel may reach another device: no remote copies, remote signals or barrier semaphores. Data moves between devices by JAX's collectives and lax.ppermute only.
A program may use at most 128 MiB of HBM per device.

v0:
```python
import jax
import jax.numpy as jnp
from jax import lax
from jax.sharding import PartitionSpec as P

PAIRS = 16


def joined_2(shard, axis, combine):
    everything = jax.tree.map(lambda part: lax.all_gather(part, axis), shard)
    initial = jax.tree.map(lambda part: part[0], everything)

    def hop(k, so_far):
        return combine(so_far, jax.tree.map(lambda part: part[k], everything))

    return lax.fori_loop(1, lax.axis_size(axis), hop, initial)


def make_fold(queries, query_norm, band_list, counts):

    def fold(state, shard_rows, offset):
        count_in = shard_rows.shape[0]
        rows_dev = shard_rows.shape[1]

        def compute(inner):
            key_rows = shard_rows.reshape(count_in * rows_dev, shard_rows.shape[2])
            key_norm = jnp.sum(key_rows * key_rows, -1)
            product = jnp.einsum("qd,kd->qk", queries, key_rows, precision=lax.Precision.HIGHEST)
            distance = query_norm[:, None] + key_norm[None, :] - 2.0 * product
            blocks = []
            for band_sq in band_list:
                scores = (-distance / (2.0 * band_sq)).reshape(
                    distance.shape[0], count_in, rows_dev
                )
                peak = jnp.max(scores, -1)
                blocks.append(peak + jnp.log(jnp.sum(jnp.exp(scores - peak[..., None]), -1)))
            update = jnp.stack(blocks)
            return lax.dynamic_update_slice(inner, update, (0, 0, offset))

        needed = jnp.any(counts > 0)
        return lax.cond(needed, compute, lambda inner: inner, state)

    return fold


def per_device(samples, pair_table, assignment, band_index):
    local_subs, rows_dev, width = samples.shape
    rounds = assignment.shape[0]
    group_size = lax.axis_size("grp")
    group_index = lax.axis_index("grp")
    members = local_subs * lax.axis_size("blk")
    band_sq = width * (1.0 + band_index.astype(jnp.float32) / 256.0) / 32.0
    local_pick = assignment - group_index * rows_dev
    onehot = (
        local_pick[:, :, None] == jnp.arange(rows_dev, dtype=jnp.int32)[None, None, :]
    ).astype(jnp.float32)
    picked = jnp.einsum("tsr,srd->td", onehot, samples, precision=lax.Precision.HIGHEST)
    centre = lax.psum(picked, ("blk", "grp")) / members
    member_ids = jnp.arange(members, dtype=jnp.int32)
    count_int = jnp.sum(
        (pair_table[:, :, None] == member_ids[None, None, :]).astype(jnp.int32), axis=1
    )
    counts = count_int.astype(jnp.float32)
    gathered = lax.all_gather(samples, "grp", axis=1, tiled=True)
    query_count = local_subs * rows_dev * group_size
    queries = gathered.reshape(query_count, width)
    query_norm = jnp.sum(queries * queries, -1)
    start_state = jnp.zeros((rounds, query_count, members), jnp.float32)
    fold = make_fold(queries, query_norm, [band_sq[turn] for turn in range(rounds)], count_int)
    partial_value = fold(
        start_state, lax.all_gather(samples, "blk", axis=0, tiled=True), jnp.int32(0)
    )
    split_view = partial_value.reshape(rounds, local_subs, group_size, rows_dev, members)
    swapped = lax.all_to_all(split_view, "grp", split_axis=2, concat_axis=2, tiled=True)
    peak = jnp.max(swapped, 2)
    kernel = peak + jnp.log(jnp.sum(jnp.exp(swapped - peak[:, :, None]), 2))
    weighted = jnp.einsum("tsrm,sm->tsr", kernel, counts, precision=lax.Precision.HIGHEST) / PAIRS
    spread = samples[None] - centre[:, None, None, :]
    logits = weighted - jnp.sum(spread * spread, -1) / (2.0 * band_sq[:, None, None])
    row_peak = jnp.max(logits, -1)
    row_total = jnp.sum(jnp.exp(logits - row_peak[..., None]), -1)

    def combine_pair(first, second):
        joined = jnp.maximum(first[0], second[0])
        return (
            joined,
            first[1] * jnp.exp(first[0] - joined) + second[1] * jnp.exp(second[0] - joined),
        )

    peak_all, total_all = joined_2((row_peak, row_total), "grp", combine_pair)
    return logits - peak_all[..., None] - jnp.log(total_all)[..., None]


def solution(mesh):
    return jax.shard_map(
        per_device,
        mesh=mesh,
        in_specs=(P("blk", "grp", None), P("blk", None), P(None, "blk"), P()),
        out_specs=P(None, "blk", "grp"),
        check_vma=False,
    )
```

profile of v0, /device:TPU:0, one launch (start us, length us, event | category | flops | bytes accessed | tf_op | source)
XLA Modules:
  0.0 123.1 jit_solution(9642932200936565193)
XLA Ops:
  6.5 0.0 all-gather.6.cloned.1.call-start
  6.5 0.7 all-gather.6.cloned.1.call-update
  7.3 0.8 convert_reduce_fusion
  8.0 0.6 compare_reduce_fusion
  9.3 0.7 broadcast_subtract_fusion
  10.0 0.1 copy.19
  10.1 1.2 convolution_bitcast_fusion
  11.3 42.0 %psum.7 = f32[2,256]{1,0:T(2,128)S(1)} all-reduce(f32[2,256]{1,0:T(2,128)S(1)} %convolution_bitcast_fusion), channel_id=1, replica_groups=mesh['blk'=8,'grp'=4] {'blk','grp'}, use_global_device_ids=true, to_apply=%region_12.0 | all-reduce | flops 512 | bytes 4096 | tf_op jit(solution)/shard_map/psum | solution.py:58
  53.2 15.9 %all_gather.18 = f32[4,128,256]{2,1,0:T(8,128)S(1)} all-gather(f32[4,32,256]{2,1,0:T(8,128)} %param.8), channel_id=1, replica_groups=mesh['blk'=8,'grp'=4] {'grp'}, dimensions={1}, use_global_device_ids=true | all-gather | bytes 655360 | tf_op jit(solution)/shard_map/all_gather | solution.py:64
  69.2 0.7 multiply_add_fusion
  69.8 0.0 all-gather.6.cloned.1.call-done
  69.8 14.7 %conditional.1 = (f32[2,512,32]{1,2,0:T(8,128)S(1)}) conditional(s32[]{:T(128)} %convert_element_type.15, () %tuple.36, (f32[4,128,256]{2,1,0:T(8,128)S(1)}, f32[32,32,256]{2,1,0:T(8,128)}, f32[2]{0:T(128)S(1)}) %tuple.37), branch_computations={%region_2.0_spmd, %region_3.10_spmd} | conditional | flops 1617689088 | bytes 25186376 | solution.py:41
  69.8 1.4 %multiply_reduce_fusion = f32[32,32]{1,0:T(8,128)S(1)} fusion(f32[32,32,256]{2,1,0:T(8,128)} %get-tuple-element.164), kind=kLoop, calls=%fused_computation.11 | loop fusion | flops 523264 | bytes 1052672 | tf_op jit(solution)/shard_map/cond/branch_1_fun/reduce_sum | solution.py:27
  71.3 0.1 add.87
  71.3 0.7 fusion.12
  73.4 0.1 multiply_reduce_fusion.1
  73.5 5.3 %broadcast_divide_fusion.1 = (f32[512,1024]{1,0:T(8,128)}, f32[512,1024]{1,0:T(8,128)}) fusion(f32[]{:T(128)} %bitcast.3, f32[]{:T(128)} %bitcast.6, f32[512,256]{1,0:T(8,128)S(1)} %bitcast.71, f32[1024,256]{1,0:T(8,128)} %bitcast.74, f32[1024]{0:T(1024)S(1)} %add.87, f32[512]{0:T(512)S(1)} %bitcast.80), kind=kOutput, calls=%fused_computation.10 | convolution fusion | flops 1613758464 | bytes 5773320 | tf_op jit(solution)/shard_map/cond/branch_1_fun/qd,kd->qk/dot_general | solution.py:28
  78.8 1.9 %copy.16 = f32[512,1024]{0,1:T(8,128)S(1)} copy(f32[512,1024]{1,0:T(8,128)} %get-tuple-element.190) | data formatting | bytes 4194304 | tf_op jit(solution)/shard_map/cond/branch_1_fun/div | solution.py:32
  80.8 0.3 bitcast_reduce_fusion.1
  81.1 0.5 fusion.3
  81.6 1.9 %copy.17 = f32[512,1024]{0,1:T(8,128)S(1)} copy(f32[512,1024]{1,0:T(8,128)} %get-tuple-element.191) | data formatting | bytes 4194304 | tf_op jit(solution)/shard_map/cond/branch_1_fun/div | solution.py:32
  83.6 0.3 bitcast_reduce_fusion
  83.9 0.5 fusion.1
  84.5 0.0 copy-start
  84.5 0.3 reshape.79
  84.8 0.1 copy.28
  84.9 1.0 reshape.97
  85.9 3.8 %all-to-all-start = ((f32[4,1,8192]{2,1,0:T(1,128)}), f32[4,1,8192]{2,1,0:T(1,128)S(1)}, u32[]{:S(2)}, u32[]{:S(2)}) async-start(f32[4,1,8192]{2,1,0:T(1,128)} %reshape.97), calls=%async_computation | async-start | bytes 262144 | tf_op jit(solution)/shard_map/all_to_all | solution.py:74
  89.7 0.0 copy-done
  89.7 0.1 multiply_reduce_fusion.2
  89.8 5.8 %all-to-all-done = f32[4,1,8192]{2,1,0:T(1,128)S(1)} async-done(((f32[4,1,8192]{2,1,0:T(1,128)}), f32[4,1,8192]{2,1,0:T(1,128)S(1)}, u32[]{:S(2)}, u32[]{:S(2)}) %all-to-all-start) | async-done | bytes 131104 | tf_op jit(solution)/shard_map/all_to_all | solution.py:74
  95.6 0.5 broadcast.44
  96.1 1.0 reduce.5
  97.1 0.3 reshape.98
  97.4 0.1 bitcast_reduce_fusion.2
  97.6 0.2 exponential_reduce_fusion
  97.8 0.2 fusion.6
  98.0 0.2 fusion.11
  98.2 0.2 exponential_reduce_fusion.1
  98.3 9.0 %all-gather.3 = f32[4,2,4]{2,1,0:T(2,128)S(1)} all-gather(f32[1,2,4]{2,1,0:T(2,128)S(1)} %bitcast.79), channel_id=3, replica_groups=mesh['blk'=8,'grp'=4] {'grp'}, dimensions={0}, use_global_device_ids=true | all-gather | bytes 160 | tf_op jit(solution)/shard_map/all_gather | solution.py:10
  107.3 8.2 %all-gather.2 = f32[4,2,4]{2,1,0:T(2,128)S(1)} all-gather(f32[1,2,4]{2,1,0:T(2,128)S(1)} %bitcast.77), channel_id=2, replica_groups=mesh['blk'=8,'grp'=4] {'grp'}, dimensions={0}, use_global_device_ids=true | all-gather | bytes 160 | tf_op jit(solution)/shard_map/all_gather | solution.py:10
  115.5 0.1 while.17
  115.6 0.7 subtract_subtract_fusion
  (12 shorter events, 0.2 us)
Async XLA Ops:
  6.5 63.3 %all-gather.6.cloned.1.call-start = ((), (), s32[]{:S(2)}) async-start(), calls=%async_computation.1 | async-start | bytes 1179648 | tf_op jit(solution)/shard_map/all_gather | solution.py:71
  84.5 5.2 %copy-start = (f32[4,32,256]{2,1,0:T(8,128)S(1)}, f32[4,32,256]{2,1,0:T(8,128)}, u32[]{:S(2)}) copy-start(f32[4,32,256]{2,1,0:T(8,128)} %param.8) | copy-start | bytes 393220
  85.9 9.7 %all-to-all-start = ((f32[4,1,8192]{2,1,0:T(1,128)}), f32[4,1,8192]{2,1,0:T(1,128)S(1)}, u32[]{:S(2)}, u32[]{:S(2)}) async-start(f32[4,1,8192]{2,1,0:T(1,128)} %reshape.97), calls=%async_computation | async-start | bytes 262144 | tf_op jit(solution)/shard_map/all_to_all | solution.py:74
Sparse Core Ops, SparseCore 0:
  9.2 26.2 all-gather.5
where the time goes:
time: 124 us; the launch traced here: 123 us
  blocking collectives  75 us (60%)
  between operations  14.1 us (11%)
  other arithmetic  8.66 us (7%)
  local copies, waits for them, and re-layouts  6.86 us (6%)
  matrix products  6.7 us (5%)
  waiting for transfers between devices  6.5 us (5%)
  starting transfers between devices  3.8 us (3%)
  loops' own time  1.43 us (1%)
    psum x1, blocking collectives, per_device(): centre = lax.psum(picked, ('blk', 'grp')) / members  42 us
    all_gather x2, blocking collectives, joined_2(): everything = jax.tree.map(lambda part: lax.all_gather(part, axis), shard)  17.2 us
    all_gather x1, blocking collectives, per_device(): gathered = lax.all_gather(samples, 'grp', axis=1, tiled=True)  15.9 us
    all_to_all x1, waiting for transfers between devices, per_device(): lax.all_to_all(split_view, 'grp', split_axis=2, concat_axis=2, tiled=True)  5.79 us
    dot_general x1, matrix products, compute(): jnp.einsum('qd,kd->qk', queries, key_rows, precision=lax.Precision.HIGHEST)  5.35 us
    div x2, local copies, waits for them, and re-layouts, compute(): -distance / (2.0 * band_sq)  3.84 us
    all_to_all x1, starting transfers between devices, per_device(): lax.all_to_all(split_view, 'grp', split_axis=2, concat_axis=2, tiled=True)  3.8 us
  transfers between devices with their start and end apart: 2, of which 1 were waited for; matrix products, arithmetic and copies ran while one was open for 3% of the time, Pallas kernels for 0%

commit v1 on v0

--- a/solution.py
+++ b/solution.py
@@ -61,7 +61,12 @@
         (pair_table[:, :, None] == member_ids[None, None, :]).astype(jnp.int32), axis=1
     )
     counts = count_int.astype(jnp.float32)
-    gathered = lax.all_gather(samples, "grp", axis=1, tiled=True)
+    ring = [samples]
+    for hop_ in range(3):
+        ring.append(lax.ppermute(ring[-1], "grp", [(dev, (dev + 1) % 4) for dev in range(4)]))
+    gathered = jnp.roll(
+        jnp.concatenate(ring[::-1], axis=1), (lax.axis_index("grp") + 1) * ring[0].shape[1], axis=1
+    )
     query_count = local_subs * rows_dev * group_size
     queries = gathered.reshape(query_count, width)
     query_norm = jnp.sum(queries * queries, -1)

time: 124 us -> 119 us (0.960)
  blocking collectives: 75 us -> 57.5 us
  waiting for transfers between devices: 6.5 us -> 15 us
  starting transfers between devices: 3.8 us -> 8.27 us
    all_gather x1 -> x0, blocking collectives: 15.9 us -> none  [per_device(): gathered = lax.all_gather(samples, 'grp', axis=1, tiled=True)]
    ppermute x0 -> x3, waiting for transfers between devices: none -> 8.56 us  [per_device(): lax.ppermute(ring[-1], 'grp', [(dev, (dev + 1) % 4) for dev in range(4)])]
    ppermute x0 -> x3, starting transfers between devices: none -> 4.94 us  [per_device(): lax.ppermute(ring[-1], 'grp', [(dev, (dev + 1) % 4) for dev in range(4)])]
    psum x1, blocking collectives: 42 us -> 40.3 us  [per_device(): centre = lax.psum(picked, ('blk', 'grp')) / members]
  transfers between devices with their start and end apart: 2 -> 5, of which waited for: 1 -> 3; matrix products, arithmetic and copies ran while one was open for 3% -> 4% of each run, Pallas kernels for 0% -> 0%
where the time goes in v1:
time: 119 us
  blocking collectives  57.5 us (48%)
  waiting for transfers between devices  15 us (13%)
  between operations  14.2 us (12%)
  other arithmetic  8.77 us (7%)
  starting transfers between devices  8.27 us (7%)
  local copies, waits for them, and re-layouts  7.86 us (7%)
  matrix products  5.48 us (5%)
  loops' own time  1.4 us (1%)
    psum x1, blocking collectives, per_device(): centre = lax.psum(picked, ('blk', 'grp')) / members  40.3 us
    all_gather x2, blocking collectives, joined_2(): everything = jax.tree.map(lambda part: lax.all_gather(part, axis), shard)  17.2 us
    ppermute x3, waiting for transfers between devices, per_device(): lax.ppermute(ring[-1], 'grp', [(dev, (dev + 1) % 4) for dev in range(4)])  8.56 us
    all_to_all x1, waiting for transfers between devices, per_device(): lax.all_to_all(split_view, 'grp', split_axis=2, concat_axis=2, tiled=True)  5.74 us
    ppermute x3, starting transfers between devices, per_device(): lax.ppermute(ring[-1], 'grp', [(dev, (dev + 1) % 4) for dev in range(4)])  4.94 us
    dot_general x1, matrix products, compute(): jnp.einsum('qd,kd->qk', queries, key_rows, precision=lax.Precision.HIGHEST)  4.13 us
    div x2, local copies, waits for them, and re-layouts, compute(): -distance / (2.0 * band_sq)  3.84 us
    all_to_all x1, starting transfers between devices, per_device(): lax.all_to_all(split_view, 'grp', split_axis=2, concat_axis=2, tiled=True)  3.32 us
  transfers between devices with their start and end apart: 5, of which 3 were waited for; matrix products, arithmetic and copies ran while one was open for 4% of the time, Pallas kernels for 0%

profile of v1, /device:TPU:0, one launch (start us, length us, event | category | flops | bytes accessed | tf_op | source)
XLA Modules:
  0.0 118.5 jit_solution(1439327584571779967)
XLA Ops:
  6.5 0.0 copy-start
  6.5 0.0 all-gather.6.cloned.1.call-start
  6.5 0.7 all-gather.6.cloned.1.call-update
  7.3 3.1 %collective-permute-start = (f32[4,32,256]{2,1,0:T(8,128)}, f32[4,32,256]{2,1,0:T(8,128)S(1)}, u32[]{:S(2)}, u32[]{:S(2)}) collective-permute-start(f32[4,32,256]{2,1,0:T(8,128)} %param.8), channel_id=1, source_target_pairs={{0,1},{1,2},{2,3},{3,0},{4,5},{5,6},{6,7},{7,4},{8,9},{9,10},{10,1... | collective-permute-start | bytes 393224 | tf_op jit(solution)/shard_map/ppermute | solution.py:66
  10.4 0.7 broadcast_subtract_fusion
  11.0 0.8 convert_reduce_fusion
  11.8 4.3 %collective-permute-done = f32[4,32,256]{2,1,0:T(8,128)S(1)} collective-permute-done((f32[4,32,256]{2,1,0:T(8,128)}, f32[4,32,256]{2,1,0:T(8,128)S(1)}, u32[]{:S(2)}, u32[]{:S(2)}) %collective-permute-start) | collective-permute-done | bytes 131104 | tf_op jit(solution)/shard_map/ppermute | solution.py:66
  16.1 0.0 collective-permute-start.1
  16.1 0.6 compare_reduce_fusion
  17.4 0.1 copy.19
  17.5 1.2 convolution_bitcast_fusion
  18.7 40.3 %psum.7 = f32[2,256]{1,0:T(2,128)S(1)} all-reduce(f32[2,256]{1,0:T(2,128)S(1)} %convolution_bitcast_fusion), channel_id=1, replica_groups=mesh['blk'=8,'grp'=4] {'blk','grp'}, use_global_device_ids=true, to_apply=%region_12.13 | all-reduce | flops 512 | bytes 4096 | tf_op jit(solution)/shard_map/psum | solution.py:58
  59.0 0.0 collective-permute-done.1
  59.0 1.8 %collective-permute-start.2 = (f32[4,32,256]{2,1,0:T(8,128)S(1)}, f32[4,32,256]{2,1,0:T(8,128)S(1)}, u32[]{:S(2)}, u32[]{:S(2)}) collective-permute-start(f32[4,32,256]{2,1,0:T(8,128)S(1)} %collective-permute-done.1), channel_id=1, source_target_pairs={{0,1},{1,2},{2,3},{3,0},{4,5},{5,6},{6,7},{7,4},{8,9},{9,10},{10,1... | collective-permute-start | bytes 393224 | tf_op jit(solution)/shard_map/ppermute | solution.py:66
  60.8 0.7 multiply_add_fusion
  61.5 4.3 %collective-permute-done.2 = f32[4,32,256]{2,1,0:T(8,128)S(1)} collective-permute-done((f32[4,32,256]{2,1,0:T(8,128)S(1)}, f32[4,32,256]{2,1,0:T(8,128)S(1)}, u32[]{:S(2)}, u32[]{:S(2)}) %collective-permute-start.2) | collective-permute-done | bytes 131104 | tf_op jit(solution)/shard_map/ppermute | solution.py:66
  65.8 0.9 constant_dynamic-update-slice_fusion.4
  66.8 0.0 copy-done
  66.8 0.0 all-gather.6.cloned.1.call-done
  66.9 13.5 %conditional.1 = (f32[2,512,32]{1,2,0:T(8,128)S(1)}) conditional(s32[]{:T(128)} %convert_element_type.15, () %tuple.40, (pred[]{:T(512)}, f32[4,256,256]{2,1,0:T(8,128)S(1)}, f32[32,32,256]{2,1,0:T(8,128)}, f32[2]{0:T(128)S(1)}, pred[]{:T(512)}, /*index=5*/s32[]{:T(128)}, s32[]{:T(128)}) %tuple.45), branch_computations={%region_2.3_spmd, %region_3.10_spmd.clone} | conditional | flops 1617689088 | bytes 29905146 | solution.py:41
  66.9 0.0 copy-start.1
  66.9 0.2 multiply_reduce_fusion.1
  67.1 1.5 %multiply_reduce_fusion = f32[32,32]{1,0:T(8,128)S(1)} fusion(f32[32,32,256]{2,1,0:T(8,128)} %get-tuple-element.242), kind=kLoop, calls=%fused_computation.16 | loop fusion | flops 523264 | bytes 1052672 | tf_op jit(solution)/shard_map/cond/branch_1_fun/reduce_sum | solution.py:27
  68.6 0.1 add.126
  68.7 0.7 fusion.12
  70.6 0.0 copy-done.1
  70.6 4.1 %broadcast_divide_fusion.1 = (f32[512,1024]{1,0:T(8,128)}, f32[512,1024]{1,0:T(8,128)}) fusion(f32[]{:T(128)} %bitcast.24, f32[]{:T(128)} %bitcast.27, f32[512,256]{1,0:T(8,128)S(1)} %bitcast.85, f32[1024,256]{1,0:T(8,128)S(1)} %bitcast.82, f32[1024]{0:T(1024)S(1)} %add.126, f32[512]{0:T(512)S(1)} %bitcast.89), kind=kOutput, calls=%fused_computation.15 | convolution fusion | flops 1613758464 | bytes 5773320 | tf_op jit(solution)/shard_map/cond/branch_1_fun/qd,kd->qk/dot_general | solution.py:28
  74.7 1.9 %copy.23 = f32[512,1024]{0,1:T(8,128)S(1)} copy(f32[512,1024]{1,0:T(8,128)} %get-tuple-element.271) | data formatting | bytes 4194304 | tf_op jit(solution)/shard_map/cond/branch_1_fun/div | solution.py:32
  76.7 0.3 bitcast_reduce_fusion.1
  77.0 0.5 fusion.5
  77.5 1.9 %copy.24 = f32[512,1024]{0,1:T(8,128)S(1)} copy(f32[512,1024]{1,0:T(8,128)} %get-tuple-element.272) | data formatting | bytes 4194304 | tf_op jit(solution)/shard_map/cond/branch_1_fun/div | solution.py:32
  79.5 0.3 bitcast_reduce_fusion
  79.8 0.5 fusion.3
  80.4 0.3 reshape.88
  80.7 0.1 copy.30
  80.8 1.0 reshape.106
  81.8 3.3 %all-to-all-start = ((f32[4,1,8192]{2,1,0:T(1,128)}), f32[4,1,8192]{2,1,0:T(1,128)S(1)}, u32[]{:S(2)}, u32[]{:S(2)}) async-start(f32[4,1,8192]{2,1,0:T(1,128)} %reshape.106), calls=%async_computation | async-start | bytes 262144 | tf_op jit(solution)/shard_map/all_to_all | solution.py:79
  85.1 0.1 multiply_reduce_fusion.2
  85.3 5.7 %all-to-all-done = f32[4,1,8192]{2,1,0:T(1,128)S(1)} async-done(((f32[4,1,8192]{2,1,0:T(1,128)}), f32[4,1,8192]{2,1,0:T(1,128)S(1)}, u32[]{:S(2)}, u32[]{:S(2)}) %all-to-all-start) | async-done | bytes 131104 | tf_op jit(solution)/shard_map/all_to_all | solution.py:79
  91.0 0.5 broadcast.48
  91.5 1.0 reduce.7
  92.5 0.3 reshape.107
  92.8 0.1 bitcast_reduce_fusion.2
  92.9 0.2 exponential_reduce_fusion
  93.2 0.2 fusion.6
  93.4 0.2 fusion.11
  93.6 0.2 exponential_reduce_fusion.1
  93.7 9.0 %all-gather.3 = f32[4,2,4]{2,1,0:T(2,128)S(1)} all-gather(f32[1,2,4]{2,1,0:T(2,128)S(1)} %bitcast.88), channel_id=3, replica_groups=mesh['blk'=8,'grp'=4] {'grp'}, dimensions={0}, use_global_device_ids=true | all-gather | bytes 160 | tf_op jit(solution)/shard_map/all_gather | solution.py:10
  102.7 8.2 %all-gather.2 = f32[4,2,4]{2,1,0:T(2,128)S(1)} all-gather(f32[1,2,4]{2,1,0:T(2,128)S(1)} %bitcast.86), channel_id=2, replica_groups=mesh['blk'=8,'grp'=4] {'grp'}, dimensions={0}, use_global_device_ids=true | all-gather | bytes 160 | tf_op jit(solution)/shard_map/all_gather | solution.py:10
  110.9 0.1 while.17
  111.0 0.7 subtract_subtract_fusion
  (19 shorter events, 0.2 us)
Async XLA Ops:
  6.5 60.3 %copy-start = (f32[4,32,256]{2,1,0:T(8,128)S(1)}, f32[4,32,256]{2,1,0:T(8,128)}, u32[]{:S(2)}) copy-start(f32[4,32,256]{2,1,0:T(8,128)} %param.8) | copy-start | bytes 393220
  6.5 60.3 %all-gather.6.cloned.1.call-start = ((), (), s32[]{:S(2)}) async-start(), calls=%async_computation.1 | async-start | bytes 1179648 | tf_op jit(solution)/shard_map/all_gather | solution.py:76
  7.3 8.8 %collective-permute-start = (f32[4,32,256]{2,1,0:T(8,128)}, f32[4,32,256]{2,1,0:T(8,128)S(1)}, u32[]{:S(2)}, u32[]{:S(2)}) collective-permute-start(f32[4,32,256]{2,1,0:T(8,128)} %param.8), channel_id=1, source_target_pairs={{0,1},{1,2},{2,3},{3,0},{4,5},{5,6},{6,7},{7,4},{8,9},{9,10},{10,1... | collective-permute-start | bytes 393224 | tf_op jit(solution)/shard_map/ppermute | solution.py:66
  16.1 42.9 %collective-permute-start.1 = (f32[4,32,256]{2,1,0:T(8,128)S(1)}, f32[4,32,256]{2,1,0:T(8,128)S(1)}, u32[]{:S(2)}, u32[]{:S(2)}) collective-permute-start(f32[4,32,256]{2,1,0:T(8,128)S(1)} %collective-permute-done), channel_id=1, source_target_pairs={{0,1},{1,2},{2,3},{3,0},{4,5},{5,6},{6,7},{7,4},{8,9},{9,10},{10,1... | collective-permute-start | bytes 393224 | tf_op jit(solution)/shard_map/ppermute | solution.py:66
  59.0 6.8 %collective-permute-start.2 = (f32[4,32,256]{2,1,0:T(8,128)S(1)}, f32[4,32,256]{2,1,0:T(8,128)S(1)}, u32[]{:S(2)}, u32[]{:S(2)}) collective-permute-start(f32[4,32,256]{2,1,0:T(8,128)S(1)} %collective-permute-done.1), channel_id=1, source_target_pairs={{0,1},{1,2},{2,3},{3,0},{4,5},{5,6},{6,7},{7,4},{8,9},{9,10},{10,1... | collective-permute-start | bytes 393224 | tf_op jit(solution)/shard_map/ppermute | solution.py:66
  66.9 3.7 %copy-start.1 = (f32[32,32,256]{2,1,0:T(8,128)S(1)}, f32[32,32,256]{2,1,0:T(8,128)}, u32[]{:S(2)}) copy-start(f32[32,32,256]{2,1,0:T(8,128)} %get-tuple-element.242) | copy-start | bytes 3145732 | tf_op jit(solution)/shard_map/cond
  81.8 9.2 %all-to-all-start = ((f32[4,1,8192]{2,1,0:T(1,128)}), f32[4,1,8192]{2,1,0:T(1,128)S(1)}, u32[]{:S(2)}, u32[]{:S(2)}) async-start(f32[4,1,8192]{2,1,0:T(1,128)} %reshape.106), calls=%async_computation | async-start | bytes 262144 | tf_op jit(solution)/shard_map/all_to_all | solution.py:79
Sparse Core Ops, SparseCore 0:
  9.2 26.4 all-gather.5
